TPU v7x, 32 devices: a whole 2x2x4 slice. The times are simulated.
32 devices in a mesh: rep: 8 (over y, x, core), tp: 4 (over z).
Axes of the slice: x: 2, y: 2, z: 4, core: 2. Of those that a mesh axis runs over, the one named last changes fastest.
Arguments:
- hidden: bfloat16 [512, 8192], P('rep'), may hold values from -6 to 6
- norm_gain: bfloat16 [8192], replicated, may hold values from 0.5 to 1.5
- query_weight_matrix: bfloat16 [8192, 4096], P(None, 'tp'), may hold values from -0.0625 to 0.0625
- key_value_weight: bfloat16 [2, 8192, 1024], P(None, None, 'tp'), may hold values from -0.0625 to 0.0625
- output_weight_matrix: bfloat16 [4096, 8192], P('tp'), may hold values from -0.375 to 0.375
- input_down_factors: bfloat16 [3, 8192, 64], P(None, ('rep', 'tp')), may hold values from -0.0625 to 0.0625
- query_up_factor: bfloat16 [64, 4096], P(None, ('rep', 'tp')), may hold values from -0.75 to 0.75
- key_value_up_factors: bfloat16 [2, 64, 1024], P(None, None, ('rep', 'tp')), may hold values from -0.75 to 0.75
- output_down_factor: bfloat16 [4096, 64], P(('rep', 'tp')), may hold values from -0.375 to 0.375
- output_up_factor: bfloat16 [64, 8192], P(None, ('rep', 'tp')), may hold values from -0.75 to 0.75
- cache_keys: bfloat16 [512, 8, 128, 128], P('rep', 'tp'), may hold values from -360 to 360
- cache_values: bfloat16 [512, 8, 128, 128], P('rep', 'tp'), may hold values from -6 to 6
- lengths: int32 [512], P('rep'), may hold values from 1 to 127
Outputs:
- attn_out: bfloat16 [512, 8192], P('rep', 'tp')
All inputs are finite; a program needn't handle non-finite values.
Results may differ from a plain program's by a relative error of at most 0.03.
Values may be sent and summed in bfloat16 or wider, within the bound.
A program may use at most 128 MiB of HBM per device.

v0:
```python
import math
import jax
import jax.numpy as jnp
from jax import lax
from jax.sharding import PartitionSpec as P

epsilon = 1e-06
rope_base = 1000000.0
adapter_scale = 0.5


def rope_angles(lengths, head_dim):
    half_dim = head_dim // 2
    frequency = rope_base ** (-(jnp.arange(half_dim, dtype=jnp.float32) * 2.0) / head_dim)
    return lengths.astype(jnp.float32)[:, None] * frequency[None, :]


def rotate(vectors, angles):
    half_dim = vectors.shape[-1] // 2
    cosine = jnp.cos(angles)[:, None, :]
    sine_part = jnp.sin(angles)[:, None, :]
    low_half = vectors[..., :half_dim]
    high_half = vectors[..., half_dim:]
    return jnp.concatenate(
        [low_half * cosine - high_half * sine_part, high_half * cosine + low_half * sine_part],
        axis=-1,
    )


def adapted(normed, frozen_matrix, inner_part, up_factor):
    base_part = jnp.dot(normed, frozen_matrix, preferred_element_type=jnp.float32)
    return base_part + adapter_scale * jnp.dot(
        inner_part, up_factor, preferred_element_type=jnp.float32
    )


def attend(query, new_key, new_value, keys, values, lengths):
    score_scale = 1.0 / math.sqrt(keys.shape[-1])
    scores = (
        jnp.einsum(
            "bkgd,bkld->bkgl", query, keys.astype(jnp.float32), precision=lax.Precision.HIGHEST
        )
        * score_scale
    )
    own_score = jnp.sum(query * new_key.astype(jnp.float32)[:, :, None, :], axis=-1) * score_scale
    live_mask = (
        jnp.arange(keys.shape[2], dtype=jnp.int32)[None, None, None, :]
        < lengths[:, None, None, None]
    )
    row_max = jnp.maximum(jnp.max(jnp.where(live_mask, scores, -1e30), axis=-1), own_score)
    weights = jnp.where(live_mask, jnp.exp(scores - row_max[..., None]), 0.0)
    own_weight = jnp.exp(own_score - row_max)
    denom_sum = jnp.sum(weights, axis=-1) + own_weight
    probs = (weights / denom_sum[..., None]).astype(jnp.bfloat16)
    own_prob = (own_weight / denom_sum).astype(jnp.bfloat16)
    context = jnp.einsum("bkgl,bkld->bkgd", probs, values, preferred_element_type=jnp.float32)
    context = (
        context
        + own_prob.astype(jnp.float32)[..., None] * new_value.astype(jnp.float32)[:, :, None, :]
    )
    return context.astype(jnp.bfloat16)


def regroup(factor, tp_count, group):
    count, rank_dim, wide = factor.shape
    return factor.reshape(count, rank_dim, tp_count, group, wide // (tp_count * group))


def settle(factor):
    count, rank_dim, tp_count, group, piece = factor.shape
    return jnp.swapaxes(factor, 2, 3).reshape(count, rank_dim, group * tp_count * piece)


def local(
    hidden,
    norm_gain,
    query_weight_matrix,
    key_value_weight,
    output_weight_matrix,
    input_down_factors,
    query_up_factor,
    key_value_up_factors,
    output_down_factor,
    output_up_factor,
    cache_keys,
    cache_values,
    lengths,
):
    states = hidden.astype(jnp.float32)
    square = jnp.mean(states * states, axis=-1, keepdims=True)
    normed = (states * lax.rsqrt(square + epsilon) * norm_gain.astype(jnp.float32)).astype(
        jnp.bfloat16
    )
    seq_count = hidden.shape[0]
    block_rows = input_down_factors.shape[1]
    rep_count = lax.axis_size("rep")
    tp_count = lax.axis_size("tp")
    tp_index = lax.axis_index("tp")
    own_features = lax.dynamic_slice_in_dim(
        normed.reshape(seq_count, rep_count, tp_count, block_rows), tp_index, 1, 2
    )
    own_features = own_features.reshape(seq_count, rep_count * block_rows)
    partial_inner = jnp.einsum(
        "bd,jdr->jbr",
        own_features,
        lax.all_gather(input_down_factors, "rep", axis=1, tiled=True),
        preferred_element_type=jnp.float32,
    )
    inner = lax.psum(partial_inner.astype(jnp.bfloat16), "tp")
    query_up_rows = query_up_factor[None]
    out_down_rows = jnp.swapaxes(output_down_factor, 0, 1)[None]
    out_up_rows = output_up_factor[None]
    per_rep = (
        lax.all_gather(query_up_rows, "rep", axis=2, tiled=True),
        lax.all_gather(key_value_up_factors, "rep", axis=2, tiled=True),
        lax.all_gather(out_down_rows, "rep", axis=2, tiled=True),
        lax.all_gather(out_up_rows, "rep", axis=2, tiled=True),
    )
    group = rep_count // tp_count
    arrived = (
        lax.all_to_all(
            regroup(per_rep[0], tp_count, group), "tp", split_axis=2, concat_axis=2, tiled=True
        ),
        lax.all_to_all(
            regroup(per_rep[1], tp_count, group), "tp", split_axis=2, concat_axis=2, tiled=True
        ),
        lax.all_to_all(
            regroup(per_rep[2], tp_count, group), "tp", split_axis=2, concat_axis=2, tiled=True
        ),
        lax.all_to_all(
            regroup(per_rep[3], tp_count, group), "tp", split_axis=2, concat_axis=2, tiled=True
        ),
    )
    query_up_local = settle(arrived[0])
    key_value_up_local = settle(arrived[1])
    out_down_local = settle(arrived[2])
    out_up_local = settle(arrived[3])
    kv_local = cache_keys.shape[1]
    head_dim = cache_keys.shape[3]
    angles = rope_angles(lengths, head_dim)
    query = adapted(normed, query_weight_matrix, inner[0], query_up_local[0]).reshape(
        seq_count, -1, head_dim
    )
    query = rotate(query, angles).reshape(seq_count, kv_local, -1, head_dim)
    new_key = adapted(normed, key_value_weight[0], inner[1], key_value_up_local[0]).reshape(
        seq_count, kv_local, head_dim
    )
    new_key = rotate(new_key, angles).astype(jnp.bfloat16)
    new_value = (
        adapted(normed, key_value_weight[1], inner[2], key_value_up_local[1])
        .reshape(seq_count, kv_local, head_dim)
        .astype(jnp.bfloat16)
    )
    context = attend(query, new_key, new_value, cache_keys, cache_values, lengths).reshape(
        seq_count, -1
    )
    partial_middle = jnp.einsum(
        "bh,rh->br", context, out_down_local[0], preferred_element_type=jnp.float32
    )
    middle = lax.psum(partial_middle, "tp").astype(jnp.bfloat16)
    partial_value = jnp.dot(context, output_weight_matrix, preferred_element_type=jnp.float32)
    summed = lax.psum_scatter(
        partial_value.astype(jnp.bfloat16), "tp", scatter_dimension=1, tiled=True
    ).astype(jnp.float32)
    summed = summed + adapter_scale * jnp.dot(
        middle, out_up_local[0], preferred_element_type=jnp.float32
    )
    return summed.astype(jnp.bfloat16)


def solution(mesh):
    return jax.shard_map(
        local,
        mesh=mesh,
        in_specs=(
            P("rep", None),
            P(),
            P(None, "tp"),
            P(None, None, "tp"),
            P("tp", None),
            P(None, ("rep", "tp"), None),
            P(None, ("rep", "tp")),
            P(None, None, ("rep", "tp")),
            P(("rep", "tp"), None),
            P(None, ("rep", "tp")),
            P("rep", "tp", None, None),
            P("rep", "tp", None, None),
            P("rep"),
        ),
        out_specs=P("rep", "tp"),
        check_vma=False,
    )
```

profile of v0, /device:TPU:0, one launch (start us, length us, event | category | flops | bytes accessed | tf_op | source)
XLA Modules:
  0.0 177.4 jit_solution(7634904349694602952)
XLA Ops:
  6.5 10.9 %all_gather.17 = bf16[2,64,256]{1,2,0:T(8,128)(2,1)S(1)} all-gather(bf16[2,64,32]{1,2,0:T(8,128)(2,1)} %param.20), channel_id=1, replica_groups=mesh['rep'=8,'tp'=4] {'rep'}, dimensions={2}, use_global_device_ids=true | all-gather | bytes 73728 | tf_op jit(solution)/shard_map/all_gather | solution.py:115
  17.4 0.8 reshape.203
  18.2 4.9 %all-to-all-start.1 = ((bf16[4,2,4096]{2,1,0:T(2,128)(2,1)}), bf16[4,2,4096]{2,1,0:T(2,128)(2,1)S(1)}, u32[]{:S(2)}, u32[]{:S(2)}) async-start(bf16[4,2,4096]{2,1,0:T(2,128)(2,1)} %reshape.203), calls=%async_computation.1 | async-start | bytes 131072 | tf_op jit(solution)/shard_map/all_to_all | solution.py:124
  23.1 0.7 convert_element_type.82
  23.8 1.5 fusion.8
  25.4 1.5 fusion.10
  26.9 0.8 reshape.182
  27.7 3.0 %fusion.2 = f32[64,256]{1,0:T(8,128)S(1)} fusion(bf16[64,8192]{1,0:T(8,128)(2,1)S(1)} %fusion.10, bf16[2,8192,256]{2,1,0:T(8,128)(2,1)} %param.16), kind=kOutput, calls=%fused_computation.3 | convolution fusion | flops 268435456 | bytes 5308416 | tf_op jit(solution)/shard_map/dot_general | solution.py:31
  30.7 3.0 %fusion = f32[64,256]{1,0:T(8,128)S(1)} fusion(bf16[64,8192]{1,0:T(8,128)(2,1)S(1)} %fusion.10, bf16[2,8192,256]{2,1,0:T(8,128)(2,1)} %param.16), kind=kOutput, calls=%fused_computation.1 | convolution fusion | flops 268435456 | bytes 5308416 | tf_op jit(solution)/shard_map/dot_general | solution.py:31
  33.8 1.5 dynamic-slice_reduce_fusion
  35.5 12.6 %all_gather.15 = bf16[3,2048,64]{1,2,0:T(8,128)(2,1)S(1)} all-gather(bf16[3,256,64]{1,2,0:T(8,128)(2,1)S(1)} %copy-done), channel_id=1, replica_groups=mesh['rep'=8,'tp'=4] {'rep'}, dimensions={1}, use_global_device_ids=true | all-gather | bytes 884736 | tf_op jit(solution)/shard_map/all_gather | solution.py:106
  48.0 0.4 fusion.17
  48.8 8.3 %all-gather = bf16[64,1024]{1,0:T(8,128)(2,1)S(1)} all-gather(bf16[64,128]{1,0:T(8,128)(2,1)S(1)} %copy-done.2), channel_id=2, replica_groups=mesh['rep'=8,'tp'=4] {'rep'}, dimensions={1}, use_global_device_ids=true | all-gather | bytes 147456 | tf_op jit(solution)/shard_map/all_gather | solution.py:114
  57.1 0.7 copy.50
  57.9 19.8 %psum.14 = bf16[3,64,64]{2,1,0:T(8,128)(2,1)S(1)} all-reduce(bf16[3,64,64]{2,1,0:T(8,128)(2,1)S(1)} %fusion.17), channel_id=1, replica_groups=mesh['rep'=8,'tp'=4] {'tp'}, use_global_device_ids=true, to_apply=%region_1.0 | all-reduce | flops 12288 | bytes 49152 | tf_op jit(solution)/shard_map/psum | solution.py:109
  77.7 3.3 %all-to-all-start = ((bf16[1,64,4,2,128]{4,3,1,0,2:T(2,128)(2,1)}), bf16[1,64,4,2,128]{4,3,1,0,2:T(2,128)(2,1)S(1)}, u32[]{:S(2)}, u32[]{:S(2)}) async-start(bf16[1,64,4,2,128]{4,3,1,0,2:T(2,128)(2,1)} %copy.50), calls=%async_computation | async-start | bytes 262144 | tf_op jit(solution)/shard_map/all_to_all | solution.py:121
  82.2 4.7 %all-to-all-done = bf16[1,64,4,2,128]{4,3,1,0,2:T(2,128)(2,1)S(1)} async-done(((bf16[1,64,4,2,128]{4,3,1,0,2:T(2,128)(2,1)}), bf16[1,64,4,2,128]{4,3,1,0,2:T(2,128)(2,1)S(1)}, u32[]{:S(2)}, u32[]{:S(2)}) %all-to-all-start) | async-done | bytes 131104 | tf_op jit(solution)/shard_map/all_to_all | solution.py:121
  87.4 8.8 %fusion.11 = f32[8,8,8,128]{3,1,2,0:T(8,128)S(1)} fusion(f32[64,1024]{1,0:T(8,128)S(1)} %convolution_multiply_fusion.2, bf16[64,8192]{1,0:T(8,128)(2,1)S(1)} %fusion.10, bf16[8192,1024]{1,0:T(8,128)(2,1)} %param.15), kind=kOutput, calls=%fused_computation.19 | convolution fusion | flops 1073807360 | bytes 18350080 | tf_op jit(solution)/shard_map/dot_general | solution.py:31
  96.6 0.4 fusion.18
  97.1 8.5 %select_reduce_fusion = (f32[64,2,4]{2,1,0:T(2,128)S(1)}, f32[64,2,4,128]{3,2,1,0:T(4,128)S(1)}) fusion(pred[64,128]{1,0:T(8,128)(4,1)S(1)} %iota_compare_fusion, f32[64,2,4,128]{3,2,1,0:T(4,128)S(1)} %bitcast.58, bf16[64,2,128,128]{3,2,1,0:T(8,128)(2,1)} %param.23), kind=kOutput, calls=%fused_computation.34 | convolution fusion | flops 100859392 | bytes 4728832 | tf_op jit(solution)/shard_map/bkgd,bkld->bkgl/dot_general | solution.py:40
  105.8 0.4 fusion.19
  106.6 3.5 %fusion.12 = bf16[64,2,4,128]{3,2,1,0:T(4,128)(2,1)S(1)} fusion(bf16[64,2,128,128]{3,2,1,0:T(8,128)(2,1)} %param.24, f32[64,2,4,128]{3,2,1,0:T(4,128)S(1)} %get-tuple-element.16, f32[64,2,128]{2,1,0:T(2,128)S(1)} %reshape.192, f32[64,2,4]{2,1,0:T(2,128)S(1)} %copy.59, f32[64,2,4]{2,1,0:T(2,128)S(1)} %copy.58, f32[64,2,4]{2,1,0:T(2,128)S(1)} %copy.56, ...), kind=kOutput, calls=%fused_computation.20 | convolution fusion | flops 17235968 | bytes 4667392 | tf_op jit(solution)/shard_map/bkgl,bkld->bkgd/dot_general | solution.py:56
  110.2 9.8 %convolution_convert_fusion = bf16[64,8192]{1,0:T(8,128)(2,1)} fusion(bf16[64,1024]{1,0:T(8,128)(2,1)S(1)} %reshape.189, bf16[1024,8192]{1,0:T(8,128)(2,1)} %param.17), kind=kOutput, calls=%fused_computation | convolution fusion | flops 1074266112 | bytes 17956864 | tf_op jit(solution)/shard_map/dot_general | solution.py:161
  120.0 8.2 %all-gather.1 = bf16[64,1024]{1,0:T(8,128)(2,1)S(1)} all-gather(bf16[64,128]{1,0:T(8,128)(2,1)S(1)} %bitcast.66), channel_id=3, replica_groups=mesh['rep'=8,'tp'=4] {'rep'}, dimensions={1}, use_global_device_ids=true | all-gather | bytes 147456 | tf_op jit(solution)/shard_map/all_gather | solution.py:116
  128.2 0.7 copy.61
  129.0 3.3 %all-to-all-start.2 = ((bf16[1,64,4,2,128]{4,3,1,0,2:T(2,128)(2,1)}), bf16[1,64,4,2,128]{4,3,1,0,2:T(2,128)(2,1)S(1)}, u32[]{:S(2)}, u32[]{:S(2)}) async-start(bf16[1,64,4,2,128]{4,3,1,0,2:T(2,128)(2,1)} %copy.61), calls=%async_computation.3 | async-start | bytes 262144 | tf_op jit(solution)/shard_map/all_to_all | solution.py:127
  132.3 9.8 %all-gather.2 = bf16[64,2048]{1,0:T(8,128)(2,1)S(1)} all-gather(bf16[64,256]{1,0:T(8,128)(2,1)S(1)} %copy-done.1), channel_id=4, replica_groups=mesh['rep'=8,'tp'=4] {'rep'}, dimensions={1}, use_global_device_ids=true | all-gather | bytes 294912 | tf_op jit(solution)/shard_map/all_gather | solution.py:117
  142.2 0.9 copy.63
  143.1 5.0 %all-to-all-start.3 = ((bf16[1,64,4,2,256]{4,3,1,0,2:T(2,128)(2,1)}), bf16[1,64,4,2,256]{4,3,1,0,2:T(2,128)(2,1)S(1)}, u32[]{:S(2)}, u32[]{:S(2)}) async-start(bf16[1,64,4,2,256]{4,3,1,0,2:T(2,128)(2,1)} %copy.63), calls=%async_computation.4 | async-start | bytes 524288 | tf_op jit(solution)/shard_map/all_to_all | solution.py:130
  148.6 19.5 %psum.15 = bf16[64,64]{1,0:T(8,128)(2,1)S(1)} all-reduce(f32[64,64]{1,0:T(8,128)S(1)} %fusion.29), channel_id=1, replica_groups=mesh['rep'=8,'tp'=4] {'tp'}, use_global_device_ids=true, to_apply=%region_6.7 | all-reduce | flops 4096 | bytes 24576 | tf_op jit(solution)/shard_map/psum | solution.py:160
  168.1 0.3 copy.64
  168.7 1.9 %fusion.7 = bf16[64,2048]{1,0:T(8,128)(2,1)} fusion(bf16[64,2048]{1,0:T(8,128)(2,1)S(1)} %squeeze_reshape.11, bf16[64,2048]{1,0:T(8,128)(2,1)} %reduce-scatter.2.cloned.1.call-done, bf16[64,64]{1,0:T(8,128)(2,1)S(1)} %psum.15), kind=kOutput, calls=%fused_computation.11 | convolution fusion | flops 17301504 | bytes 794624 | tf_op jit(solution)/shard_map/dot_general | solution.py:165
  (56 shorter events, 4.0 us)
Async XLA Ops:
  18.2 59.5 %all-to-all-start.1 = ((bf16[4,2,4096]{2,1,0:T(2,128)(2,1)}), bf16[4,2,4096]{2,1,0:T(2,128)(2,1)S(1)}, u32[]{:S(2)}, u32[]{:S(2)}) async-start(bf16[4,2,4096]{2,1,0:T(2,128)(2,1)} %reshape.203), calls=%async_computation.1 | async-start | bytes 131072 | tf_op jit(solution)/shard_map/all_to_all | solution.py:124
  30.7 4.7 %copy-start = (bf16[3,256,64]{1,2,0:T(8,128)(2,1)S(1)}, bf16[3,256,64]{1,2,0:T(8,128)(2,1)}, u32[]{:S(2)}) copy-start(bf16[3,256,64]{1,2,0:T(8,128)(2,1)} %param.18) | copy-start | bytes 294916
  30.7 17.3 %copy-start.4 = (s32[64]{0:T(128)S(1)}, s32[64]{0:T(128)}, u32[]{:S(2)}) copy-start(s32[64]{0:T(128)} %param.25) | copy-start | bytes 772
  30.7 18.0 %copy-start.2 = (bf16[64,128]{1,0:T(8,128)(2,1)S(1)}, bf16[64,128]{1,0:T(8,128)(2,1)}, u32[]{:S(2)}) copy-start(bf16[64,128]{1,0:T(8,128)(2,1)} %param.19) | copy-start | bytes 49156
  77.7 9.2 %all-to-all-start = ((bf16[1,64,4,2,128]{4,3,1,0,2:T(2,128)(2,1)}), bf16[1,64,4,2,128]{4,3,1,0,2:T(2,128)(2,1)S(1)}, u32[]{:S(2)}, u32[]{:S(2)}) async-start(bf16[1,64,4,2,128]{4,3,1,0,2:T(2,128)(2,1)} %copy.50), calls=%async_computation | async-start | bytes 262144 | tf_op jit(solution)/shard_map/all_to_all | solution.py:121
  81.1 87.6 %reduce-scatter.2.cloned.1.call-start = ((), (), s32[]{:S(2)}) async-start(), calls=%async_computation.5 | async-start | bytes 1310720 | tf_op jit(solution)/shard_map/reduce_scatter | solution.py:162
  110.2 9.8 %copy-start.3 = (bf16[128,64]{0,1:T(8,128)(2,1)S(1)}, bf16[128,64]{0,1:T(8,128)(2,1)}, u32[]{:S(2)}) copy-start(bf16[128,64]{0,1:T(8,128)(2,1)} %param.21) | copy-start | bytes 49156
  110.2 22.1 %copy-start.1 = (bf16[64,256]{1,0:T(8,128)(2,1)S(1)}, bf16[64,256]{1,0:T(8,128)(2,1)}, u32[]{:S(2)}) copy-start(bf16[64,256]{1,0:T(8,128)(2,1)} %param.22) | copy-start | bytes 98308
  129.0 14.2 %all-to-all-start.2 = ((bf16[1,64,4,2,128]{4,3,1,0,2:T(2,128)(2,1)}), bf16[1,64,4,2,128]{4,3,1,0,2:T(2,128)(2,1)S(1)}, u32[]{:S(2)}, u32[]{:S(2)}) async-start(bf16[1,64,4,2,128]{4,3,1,0,2:T(2,128)(2,1)} %copy.61), calls=%async_computation.3 | async-start | bytes 262144 | tf_op jit(solution)/shard_map/all_to_all | solution.py:127
  143.1 25.0 %all-to-all-start.3 = ((bf16[1,64,4,2,256]{4,3,1,0,2:T(2,128)(2,1)}), bf16[1,64,4,2,256]{4,3,1,0,2:T(2,128)(2,1)S(1)}, u32[]{:S(2)}, u32[]{:S(2)}) async-start(bf16[1,64,4,2,256]{4,3,1,0,2:T(2,128)(2,1)} %copy.63), calls=%async_computation.4 | async-start | bytes 524288 | tf_op jit(solution)/shard_map/all_to_all | solution.py:130
Sparse Core Ops, SparseCore 0:
  120.1 27.4 reduce-scatter.1
where the time goes:
time: 178 us; the launch traced here: 177 us
  blocking collectives  89 us (50%)
  matrix products  39.5 us (22%)
  starting transfers between devices  16.8 us (9%)
  between operations  13.8 us (8%)
  local copies, waits for them, and re-layouts  7.97 us (4%)
  other arithmetic  5.58 us (3%)
  waiting for transfers between devices  4.78 us (3%)
    psum x1, blocking collectives, local(): inner = lax.psum(partial_inner.astype(jnp.bfloat16), 'tp')  19.8 us
    psum x1, blocking collectives, local(): middle = lax.psum(partial_middle, 'tp').astype(jnp.bfloat16)  19.5 us
    dot_general x3, matrix products, adapted(): jnp.dot(normed, frozen_matrix, preferred_element_type=jnp.float32)  14.8 us
    all_gather x1, blocking collectives, local(): lax.all_gather(input_down_factors, 'rep', axis=1, tiled=True)  12.6 us
    all_gather x1, blocking collectives, local(): lax.all_gather(key_value_up_factors, 'rep', axis=2, tiled=True)  10.9 us
    dot_general x1, matrix products, local(): jnp.dot(context, output_weight_matrix, preferred_element_type=jnp.float32)  9.79 us
    all_gather x1, blocking collectives, local(): lax.all_gather(out_up_rows, 'rep', axis=2, tiled=True)  9.75 us
    dot_general x1, matrix products, attend(): jnp.einsum('bkgd,bkld->bkgl', query, keys.astype(jnp.float32), precision=...  8.5 us
  transfers between devices with their start and end apart: 5, of which 1 were waited for; matrix products, arithmetic and copies ran while one was open for 10% of the time, Pallas kernels for 0%

commit v1 on v0

--- a/solution.py
+++ b/solution.py
@@ -114,7 +114,7 @@
         lax.all_gather(query_up_rows, "rep", axis=2, tiled=True),
         lax.all_gather(key_value_up_factors, "rep", axis=2, tiled=True),
         lax.all_gather(out_down_rows, "rep", axis=2, tiled=True),
-        lax.all_gather(out_up_rows, "rep", axis=2, tiled=True),
+        jnp.concatenate(lax.all_gather(out_up_rows, "rep"), axis=2),
     )
     group = rep_count // tp_count
     arrived = (

time: 178 us -> 178 us (level)
  transfers between devices with their start and end apart: 5 -> 5, of which waited for: 1 -> 2; matrix products, arithmetic and copies ran while one was open for 10% -> 9% of each run, Pallas kernels for 0% -> 0%
where the time goes in v1:
time: 178 us; the launch traced here: 177 us
  blocking collectives  89.4 us (50%)
  matrix products  39.5 us (22%)
  starting transfers between devices  16.2 us (9%)
  between operations  13.8 us (8%)
  local copies, waits for them, and re-layouts  6.78 us (4%)
  other arithmetic  5.58 us (3%)
  waiting for transfers between devices  5.41 us (3%)
    psum x1, blocking collectives, local(): inner = lax.psum(partial_inner.astype(jnp.bfloat16), 'tp')  19.8 us
    psum x1, blocking collectives, local(): middle = lax.psum(partial_middle, 'tp').astype(jnp.bfloat16)  19.5 us
    dot_general x3, matrix products, adapted(): jnp.dot(normed, frozen_matrix, preferred_element_type=jnp.float32)  14.8 us
    all_gather x1, blocking collectives, local(): lax.all_gather(input_down_factors, 'rep', axis=1, tiled=True)  12.6 us
    all_gather x1, blocking collectives, local(): lax.all_gather(key_value_up_factors, 'rep', axis=2, tiled=True)  10.9 us
    all_gather x1, blocking collectives, local(): lax.all_gather(out_up_rows, 'rep')  10.2 us
    dot_general x1, matrix products, local(): jnp.dot(context, output_weight_matrix, preferred_element_type=jnp.float32)  9.79 us
    dot_general x1, matrix products, attend(): jnp.einsum('bkgd,bkld->bkgl', query, keys.astype(jnp.float32), precision=...  8.5 us
  transfers between devices with their start and end apart: 5, of which 2 were waited for; matrix products, arithmetic and copies ran while one was open for 9% of the time, Pallas kernels for 0%

profile of v1, /device:TPU:0, one launch (start us, length us, event | category | flops | bytes accessed | tf_op | source)
XLA Modules:
  0.0 176.7 jit_solution(2396097959677634321)
XLA Ops:
  6.5 10.9 %all_gather.17 = bf16[2,64,256]{1,2,0:T(8,128)(2,1)S(1)} all-gather(bf16[2,64,32]{1,2,0:T(8,128)(2,1)} %param.20), channel_id=1, replica_groups=mesh['rep'=8,'tp'=4] {'rep'}, dimensions={2}, use_global_device_ids=true | all-gather | bytes 73728 | tf_op jit(solution)/shard_map/all_gather | solution.py:115
  17.4 0.8 reshape.202
  18.2 4.9 %all-to-all-start.1 = ((bf16[4,2,4096]{2,1,0:T(2,128)(2,1)}), bf16[4,2,4096]{2,1,0:T(2,128)(2,1)S(1)}, u32[]{:S(2)}, u32[]{:S(2)}) async-start(bf16[4,2,4096]{2,1,0:T(2,128)(2,1)} %reshape.202), calls=%async_computation.1 | async-start | bytes 131072 | tf_op jit(solution)/shard_map/all_to_all | solution.py:124
  23.1 0.7 convert_element_type.82
  23.8 1.5 fusion.8
  25.4 1.5 fusion.10
  26.9 0.8 reshape.182
  27.7 3.0 %fusion.2 = f32[64,256]{1,0:T(8,128)S(1)} fusion(bf16[64,8192]{1,0:T(8,128)(2,1)S(1)} %fusion.10, bf16[2,8192,256]{2,1,0:T(8,128)(2,1)} %param.16), kind=kOutput, calls=%fused_computation.3 | convolution fusion | flops 268435456 | bytes 5308416 | tf_op jit(solution)/shard_map/dot_general | solution.py:31
  30.7 3.0 %fusion = f32[64,256]{1,0:T(8,128)S(1)} fusion(bf16[64,8192]{1,0:T(8,128)(2,1)S(1)} %fusion.10, bf16[2,8192,256]{2,1,0:T(8,128)(2,1)} %param.16), kind=kOutput, calls=%fused_computation.1 | convolution fusion | flops 268435456 | bytes 5308416 | tf_op jit(solution)/shard_map/dot_general | solution.py:31
  33.8 1.5 dynamic-slice_reduce_fusion
  35.5 12.6 %all_gather.15 = bf16[3,2048,64]{1,2,0:T(8,128)(2,1)S(1)} all-gather(bf16[3,256,64]{1,2,0:T(8,128)(2,1)S(1)} %copy-done), channel_id=1, replica_groups=mesh['rep'=8,'tp'=4] {'rep'}, dimensions={1}, use_global_device_ids=true | all-gather | bytes 884736 | tf_op jit(solution)/shard_map/all_gather | solution.py:106
  48.0 0.4 fusion.17
  48.8 8.3 %all-gather = bf16[64,1024]{1,0:T(8,128)(2,1)S(1)} all-gather(bf16[64,128]{1,0:T(8,128)(2,1)S(1)} %copy-done.2), channel_id=2, replica_groups=mesh['rep'=8,'tp'=4] {'rep'}, dimensions={1}, use_global_device_ids=true | all-gather | bytes 147456 | tf_op jit(solution)/shard_map/all_gather | solution.py:114
  57.1 0.7 copy.55
  57.9 19.8 %psum.14 = bf16[3,64,64]{2,1,0:T(8,128)(2,1)S(1)} all-reduce(bf16[3,64,64]{2,1,0:T(8,128)(2,1)S(1)} %fusion.17), channel_id=1, replica_groups=mesh['rep'=8,'tp'=4] {'tp'}, use_global_device_ids=true, to_apply=%region_1.0 | all-reduce | flops 12288 | bytes 49152 | tf_op jit(solution)/shard_map/psum | solution.py:109
  77.7 3.3 %all-to-all-start = ((bf16[1,64,4,2,128]{4,3,1,0,2:T(2,128)(2,1)}), bf16[1,64,4,2,128]{4,3,1,0,2:T(2,128)(2,1)S(1)}, u32[]{:S(2)}, u32[]{:S(2)}) async-start(bf16[1,64,4,2,128]{4,3,1,0,2:T(2,128)(2,1)} %copy.55), calls=%async_computation | async-start | bytes 262144 | tf_op jit(solution)/shard_map/all_to_all | solution.py:121
  81.1 0.2 reduce-scatter.2.cloned.1.call-start
  82.2 4.7 %all-to-all-done = bf16[1,64,4,2,128]{4,3,1,0,2:T(2,128)(2,1)S(1)} async-done(((bf16[1,64,4,2,128]{4,3,1,0,2:T(2,128)(2,1)}), bf16[1,64,4,2,128]{4,3,1,0,2:T(2,128)(2,1)S(1)}, u32[]{:S(2)}, u32[]{:S(2)}) %all-to-all-start) | async-done | bytes 131104 | tf_op jit(solution)/shard_map/all_to_all | solution.py:121
  87.4 8.8 %fusion.11 = f32[8,8,8,128]{3,1,2,0:T(8,128)S(1)} fusion(f32[64,1024]{1,0:T(8,128)S(1)} %convolution_multiply_fusion.2, bf16[64,8192]{1,0:T(8,128)(2,1)S(1)} %fusion.10, bf16[8192,1024]{1,0:T(8,128)(2,1)} %param.15), kind=kOutput, calls=%fused_computation.19 | convolution fusion | flops 1073807360 | bytes 18350080 | tf_op jit(solution)/shard_map/dot_general | solution.py:31
  96.6 0.4 fusion.18
  97.1 8.5 %select_reduce_fusion = (f32[64,2,4]{2,1,0:T(2,128)S(1)}, f32[64,2,4,128]{3,2,1,0:T(4,128)S(1)}) fusion(pred[64,128]{1,0:T(8,128)(4,1)S(1)} %iota_compare_fusion, f32[64,2,4,128]{3,2,1,0:T(4,128)S(1)} %bitcast.65, bf16[64,2,128,128]{3,2,1,0:T(8,128)(2,1)} %param.23), kind=kOutput, calls=%fused_computation.34 | convolution fusion | flops 100859392 | bytes 4728832 | tf_op jit(solution)/shard_map/bkgd,bkld->bkgl/dot_general | solution.py:40
  105.8 0.4 fusion.19
  106.6 3.5 %fusion.12 = bf16[64,2,4,128]{3,2,1,0:T(4,128)(2,1)S(1)} fusion(bf16[64,2,128,128]{3,2,1,0:T(8,128)(2,1)} %param.24, f32[64,2,4,128]{3,2,1,0:T(4,128)S(1)} %get-tuple-element.16, f32[64,2,128]{2,1,0:T(2,128)S(1)} %reshape.192, f32[64,2,4]{2,1,0:T(2,128)S(1)} %copy.64, f32[64,2,4]{2,1,0:T(2,128)S(1)} %copy.63, f32[64,2,4]{2,1,0:T(2,128)S(1)} %copy.61, ...), kind=kOutput, calls=%fused_computation.20 | convolution fusion | flops 17235968 | bytes 4667392 | tf_op jit(solution)/shard_map/bkgl,bkld->bkgd/dot_general | solution.py:56
  110.2 9.8 %convolution_convert_fusion = bf16[64,8192]{1,0:T(8,128)(2,1)} fusion(bf16[64,1024]{1,0:T(8,128)(2,1)S(1)} %reshape.189, bf16[1024,8192]{1,0:T(8,128)(2,1)} %param.17), kind=kOutput, calls=%fused_computation | convolution fusion | flops 1074266112 | bytes 17956864 | tf_op jit(solution)/shard_map/dot_general | solution.py:161
  120.0 8.2 %all-gather.1 = bf16[64,1024]{1,0:T(8,128)(2,1)S(1)} all-gather(bf16[64,128]{1,0:T(8,128)(2,1)S(1)} %bitcast.73), channel_id=3, replica_groups=mesh['rep'=8,'tp'=4] {'rep'}, dimensions={1}, use_global_device_ids=true | all-gather | bytes 147456 | tf_op jit(solution)/shard_map/all_gather | solution.py:116
  128.2 0.7 copy.66
  129.0 3.3 %all-to-all-start.2 = ((bf16[1,64,4,2,128]{4,3,1,0,2:T(2,128)(2,1)}), bf16[1,64,4,2,128]{4,3,1,0,2:T(2,128)(2,1)S(1)}, u32[]{:S(2)}, u32[]{:S(2)}) async-start(bf16[1,64,4,2,128]{4,3,1,0,2:T(2,128)(2,1)} %copy.66), calls=%async_computation.3 | async-start | bytes 262144 | tf_op jit(solution)/shard_map/all_to_all | solution.py:127
  132.3 10.2 %all-gather.2 = bf16[512,256]{1,0:T(8,128)(2,1)} all-gather(bf16[64,256]{1,0:T(8,128)(2,1)S(1)} %copy-done.1), channel_id=4, replica_groups=mesh['rep'=8,'tp'=4] {'rep'}, dimensions={0}, use_global_device_ids=true | all-gather | bytes 294912 | tf_op jit(solution)/shard_map/all_gather | solution.py:117
  142.5 0.6 all-to-all-done.2
  143.1 4.4 %all-to-all-start.3 = ((bf16[1,64,4,2,256]{4,1,3,0,2:T(8,128)(2,1)}), bf16[1,64,4,2,256]{4,1,3,0,2:T(8,128)(2,1)S(1)}, u32[]{:S(2)}, u32[]{:S(2)}) async-start(bf16[1,64,4,2,256]{4,1,3,0,2:T(8,128)(2,1)} %bitcast.19), calls=%async_computation.4 | async-start | bytes 524288 | tf_op jit(solution)/shard_map/all_to_all | solution.py:130
  148.0 19.5 %psum.15 = bf16[64,64]{1,0:T(8,128)(2,1)S(1)} all-reduce(f32[64,64]{1,0:T(8,128)S(1)} %fusion.29), channel_id=1, replica_groups=mesh['rep'=8,'tp'=4] {'tp'}, use_global_device_ids=true, to_apply=%region_6.7 | all-reduce | flops 4096 | bytes 24576 | tf_op jit(solution)/shard_map/psum | solution.py:160
  168.0 1.9 %fusion.7 = bf16[64,2048]{1,0:T(8,128)(2,1)} fusion(bf16[64,2048]{1,0:T(8,128)(2,1)S(1)} %squeeze_reshape.11, bf16[64,2048]{1,0:T(8,128)(2,1)} %reduce-scatter.2.cloned.1.call-done, bf16[64,64]{1,0:T(8,128)(2,1)S(1)} %psum.15), kind=kOutput, calls=%fused_computation.11 | convolution fusion | flops 17301504 | bytes 794624 | tf_op jit(solution)/shard_map/dot_general | solution.py:165
  (54 shorter events, 3.8 us)
Async XLA Ops:
  18.2 59.5 %all-to-all-start.1 = ((bf16[4,2,4096]{2,1,0:T(2,128)(2,1)}), bf16[4,2,4096]{2,1,0:T(2,128)(2,1)S(1)}, u32[]{:S(2)}, u32[]{:S(2)}) async-start(bf16[4,2,4096]{2,1,0:T(2,128)(2,1)} %reshape.202), calls=%async_computation.1 | async-start | bytes 131072 | tf_op jit(solution)/shard_map/all_to_all | solution.py:124
  30.7 4.7 %copy-start = (bf16[3,256,64]{1,2,0:T(8,128)(2,1)S(1)}, bf16[3,256,64]{1,2,0:T(8,128)(2,1)}, u32[]{:S(2)}) copy-start(bf16[3,256,64]{1,2,0:T(8,128)(2,1)} %param.18) | copy-start | bytes 294916
  30.7 17.3 %copy-start.4 = (s32[64]{0:T(128)S(1)}, s32[64]{0:T(128)}, u32[]{:S(2)}) copy-start(s32[64]{0:T(128)} %param.25) | copy-start | bytes 772
  30.7 18.0 %copy-start.2 = (bf16[64,128]{1,0:T(8,128)(2,1)S(1)}, bf16[64,128]{1,0:T(8,128)(2,1)}, u32[]{:S(2)}) copy-start(bf16[64,128]{1,0:T(8,128)(2,1)} %param.19) | copy-start | bytes 49156
  77.7 9.2 %all-to-all-start = ((bf16[1,64,4,2,128]{4,3,1,0,2:T(2,128)(2,1)}), bf16[1,64,4,2,128]{4,3,1,0,2:T(2,128)(2,1)S(1)}, u32[]{:S(2)}, u32[]{:S(2)}) async-start(bf16[1,64,4,2,128]{4,3,1,0,2:T(2,128)(2,1)} %copy.55), calls=%async_computation | async-start | bytes 262144 | tf_op jit(solution)/shard_map/all_to_all | solution.py:121
  81.1 86.9 %reduce-scatter.2.cloned.1.call-start = ((), (), s32[]{:S(2)}) async-start(), calls=%async_computation.5 | async-start | bytes 1310720 | tf_op jit(solution)/shard_map/reduce_scatter | solution.py:162
  110.2 9.8 %copy-start.3 = (bf16[128,64]{0,1:T(8,128)(2,1)S(1)}, bf16[128,64]{0,1:T(8,128)(2,1)}, u32[]{:S(2)}) copy-start(bf16[128,64]{0,1:T(8,128)(2,1)} %param.21) | copy-start | bytes 49156
  110.2 22.2 %copy-start.1 = (bf16[64,256]{1,0:T(8,128)(2,1)S(1)}, bf16[64,256]{1,0:T(8,128)(2,1)}, u32[]{:S(2)}) copy-start(bf16[64,256]{1,0:T(8,128)(2,1)} %param.22) | copy-start | bytes 98308
  129.0 14.2 %all-to-all-start.2 = ((bf16[1,64,4,2,128]{4,3,1,0,2:T(2,128)(2,1)}), bf16[1,64,4,2,128]{4,3,1,0,2:T(2,128)(2,1)S(1)}, u32[]{:S(2)}, u32[]{:S(2)}) async-start(bf16[1,64,4,2,128]{4,3,1,0,2:T(2,128)(2,1)} %copy.66), calls=%async_computation.3 | async-start | bytes 262144 | tf_op jit(solution)/shard_map/all_to_all | solution.py:127
  143.1 24.4 %all-to-all-start.3 = ((bf16[1,64,4,2,256]{4,1,3,0,2:T(8,128)(2,1)}), bf16[1,64,4,2,256]{4,1,3,0,2:T(8,128)(2,1)S(1)}, u32[]{:S(2)}, u32[]{:S(2)}) async-start(bf16[1,64,4,2,256]{4,1,3,0,2:T(8,128)(2,1)} %bitcast.19), calls=%async_computation.4 | async-start | bytes 524288 | tf_op jit(solution)/shard_map/all_to_all | solution.py:130
Sparse Core Ops, SparseCore 0:
  120.1 27.4 reduce-scatter.1
